TPU v7x, 32 devices: a whole 2x2x4 slice. The times are simulated.
32 devices in a mesh: sx: 4 (over x, core), sy: 4 (over z), dp: 2 (over y).
Axes of the slice: x: 2, y: 2, z: 4, core: 2. Of those that a mesh axis runs over, the one named last changes fastest.
Arguments:
- tokens: bfloat16 [2, 8192, 1280], P('dp', ('sx', 'sy')), may hold values from -6 to 6
- lengths: int32 [2, 64], P('dp'), may hold values from 1 to 512, 8192 in all within a row
- ln_gain: float32 [1280], replicated, may hold values from 0.1 to 1.9
- w_qkv: bfloat16 [1280, 3840], P('dp'), may hold values from -4 to 4, as said below
- w_out: bfloat16 [1280, 1280], P('dp'), may hold values from -0.15625 to 0.15625
Outputs:
- hidden: bfloat16 [2, 8192, 1280], P('dp', ('sx', 'sy'))
- pooled: float32 [2, 64, 1280], P('dp')
Inputs may be any that keep to these rules, and one draw needn't show every extreme that they name: The 64 lengths of a row sum to 8192; images are packed end to end in order. `w_qkv`: columns are queries, then keys, then values, each of 16 heads of 80 columns.
All inputs are finite; a program needn't handle non-finite values.
Results may differ from a plain program's by a relative error of at most 0.0051.
Values may be sent and summed in bfloat16 or wider, within the bound.
A program may use at most 128 MiB of HBM per device.

v0:
```python
import jax
import jax.numpy as jnp
from jax import lax
from jax.sharding import PartitionSpec as P

HEADS = 16
MAXLEN = 512


def with_halo(block, sides, width):
    for axis, dim in sides:
        count = lax.axis_size(axis)
        forward = [(i, i + 1) for i in range(count - 1)]
        backward = [(target, source) for source, target in forward]
        low = lax.ppermute(
            lax.slice_in_dim(block, block.shape[dim] - width, None, axis=dim), axis, forward
        )
        high = lax.ppermute(lax.slice_in_dim(block, 0, width, axis=dim), axis, backward)
        block = jnp.concatenate([low, block, high], axis=dim)
    return block


def image_ids(lengths, positions, total):
    offsets = jnp.cumsum(lengths) - lengths
    counted = jnp.sum((offsets[None, :] <= positions[:, None]).astype(jnp.int32), axis=1) - 1
    inside = (positions >= 0) & (positions < total)
    return jnp.where(inside, counted, -1)


def normalize(rows, ln_gain):
    values = rows.astype(jnp.float32)
    center = values - jnp.mean(values, axis=-1, keepdims=True)
    spread = jnp.mean(center * center, axis=-1, keepdims=True)
    return (center * lax.rsqrt(spread + 1e-05) * ln_gain).astype(jnp.bfloat16)


def attend(queries, keys, values, q_ids, k_ids):
    length = queries.shape[0]
    heads = queries.shape[1]
    block = min(512, length)
    scale = queries.shape[2] ** (-0.5)

    def one_block(index):
        allowed = q_ids[:, None] == k_ids[None, :]

        def one_head(head):
            q_head = lax.dynamic_index_in_dim(queries, head, 1, keepdims=False)
            k_head = lax.dynamic_index_in_dim(keys, head, 1, keepdims=False)
            v_head = lax.dynamic_index_in_dim(values, head, 1, keepdims=False)
            scores = jnp.dot(q_head, k_head.T, preferred_element_type=jnp.float32) * scale
            scores = jnp.where(allowed, scores, -1e30)
            top = jnp.max(scores, axis=1, keepdims=True)
            weights = jnp.exp(scores - top)
            probs = (weights / jnp.sum(weights, axis=1, keepdims=True)).astype(jnp.bfloat16)
            return jnp.dot(probs, v_head, preferred_element_type=jnp.float32).astype(jnp.bfloat16)

        outcome = lax.map(one_head, jnp.arange(heads, dtype=jnp.int32))
        return jnp.transpose(outcome, (1, 0, 2))

    blocks = lax.map(one_block, jnp.arange(length // block, dtype=jnp.int32))
    return blocks.reshape(length, heads, -1)


def shards(tokens, lengths, ln_gain, w_qkv, w_out):
    qkv_full, out_full = (
        lax.all_gather(w_qkv, "dp", axis=0, tiled=True),
        lax.all_gather(w_out, "dp", axis=0, tiled=True),
    )
    count_rows = tokens.shape[0]
    local = tokens.shape[1]
    width = tokens.shape[2]
    size = width // HEADS
    images = lengths.shape[1]
    count_x = lax.axis_size("sx")
    count_y = lax.axis_size("sy")
    total = local * count_x * count_y
    shard = lax.axis_index("sx") * count_y + lax.axis_index("sy")
    own_positions = shard * local + jnp.arange(local, dtype=jnp.int32)
    own_list = [image_ids(lengths[0], own_positions, total)]
    normed = normalize(tokens, ln_gain)
    qkv = jnp.dot(
        normed.reshape(count_rows * local, width), qkv_full, preferred_element_type=jnp.float32
    )
    qkv = qkv.astype(jnp.bfloat16).reshape(count_rows, local, 3 * width)
    pieces = qkv.reshape(count_rows, local, 3, HEADS, size)
    keyvals = with_halo(pieces[:, :, 1:3], ((("sx", "sy"), 1),), MAXLEN)
    k_pos = shard * local - MAXLEN + jnp.arange(local + 2 * MAXLEN, dtype=jnp.int32)
    rowidx = 0
    k_ids = image_ids(lengths[rowidx], k_pos, total)
    outcomes = [
        attend(
            pieces[rowidx, :, 0],
            keyvals[rowidx, :, 0],
            keyvals[rowidx, :, 1],
            own_list[rowidx],
            k_ids,
        )
    ]
    context = jnp.stack(outcomes, axis=0).reshape(count_rows * local, width)
    mixed = jnp.dot(context, out_full, preferred_element_type=jnp.float32).reshape(
        count_rows, local, width
    )
    hidden = (tokens.astype(jnp.float32) + mixed).astype(jnp.bfloat16)
    labels = jnp.arange(images, dtype=jnp.int32)
    rowidx = 0
    onehot = (labels[:, None] == own_list[rowidx][None, :]).astype(jnp.bfloat16)
    parts_list = [jnp.dot(onehot, hidden[rowidx], preferred_element_type=jnp.float32)]
    terms = jnp.stack(parts_list, axis=0)
    sums = lax.psum(terms, ("sx", "sy"))
    pooled = sums / lengths.astype(jnp.float32)[:, :, None]
    return (hidden, pooled)


def solution(mesh):
    in_specs = (P("dp", ("sx", "sy"), None), P("dp", None), P(), P("dp", None), P("dp", None))
    out_specs = (P("dp", ("sx", "sy"), None), P("dp", None, None))
    return jax.shard_map(shards, mesh=mesh, in_specs=in_specs, out_specs=out_specs, check_vma=False)
```

profile of v0, /device:TPU:8, one launch (start us, length us, event | category | flops | bytes accessed | tf_op | source)
XLA Modules:
  0.0 491.2 jit_solution(5797661446178218919)
XLA Ops:
  9.2 123.8 %all-gather.3.cloned.1.call-done = bf16[1280,3840]{1,0:T(8,128)(2,1)} async-done(((bf16[640,3840]{1,0:T(8,128)(2,1)}), bf16[1280,3840]{1,0:T(8,128)(2,1)}) %all-gather.3.cloned.1.call-update) | async-done | bytes 9830416 | tf_op jit(solution)/shard_map/all_gather | solution.py:66
  133.0 10.9 %convolution_convert_fusion = bf16[512,3840]{1,0:T(8,128)(2,1)} fusion(bf16[1280,3840]{1,0:T(8,128)(2,1)} %all-gather.3.cloned.1.call-done, bf16[1,512,1280]{2,1,0:T(8,128)(2,1)S(1)} %copy-done, f32[1280]{0:T(1024)S(1)} %copy-done.4, f32[512]{0:T(512)S(1)} %add_rsqrt_fusion, f32[512]{0:T(512)S(1)} %broadcast_multiply_fusion), kind=kOutput, calls=%fused_computation.19 | convolution fusion | flops 5038407680 | bytes 15082496 | tf_op jit(solution)/shard_map/dot_general | solution.py:81
  144.0 6.3 %copy.10 = bf16[512,3840]{0,1:T(8,128)(2,1)} copy(bf16[512,3840]{1,0:T(8,128)(2,1)} %convolution_convert_fusion) | data formatting | bytes 7864320 | tf_op jit(solution)/shard_map/convert_element_type | solution.py:84
  150.3 1.9 slice.17
  152.2 2.5 collective-permute-start.1
  154.7 3.4 collective-permute-start
  158.7 2.5 slice_bitcast_fusion.2
  161.2 51.9 %collective-permute-done.1 = bf16[1,512,2,16,80]{1,4,3,2,0:T(8,128)(2,1)} collective-permute-done((bf16[1,512,2,16,80]{1,4,3,2,0:T(8,128)(2,1)S(1)}, bf16[1,512,2,16,80]{1,4,3,2,0:T(8,128)(2,1)}, u32[]{:S(2)}, u32[]{:S(2)}) %collective-permute-start.1) | collective-permute-done | bytes 2621472 | tf_op jit(solution)/shard_map/ppermute | solution.py:18
  213.0 28.8 %collective-permute-done = bf16[1,512,2,16,80]{1,4,3,2,0:T(8,128)(2,1)} collective-permute-done((bf16[1,512,2,16,80]{1,4,3,2,0:T(8,128)(2,1)S(1)}, bf16[1,512,2,16,80]{1,4,3,2,0:T(8,128)(2,1)}, u32[]{:S(2)}, u32[]{:S(2)}) %collective-permute-start) | collective-permute-done | bytes 2621472 | tf_op jit(solution)/shard_map/ppermute | solution.py:15
  241.8 3.4 pad_maximum_fusion
  245.3 3.4 slice_bitcast_fusion
  248.6 106.8 %while.18 = (s32[]{:T(128)}, bf16[16,512,80]{1,2,0:T(8,128)(2,1)S(1)}, s32[16]{0:T(128)S(1)}, bf16[512,16,80]{0,2,1:T(8,128)(2,1)}, bf16[1536,16,80]{0,2,1:T(8,1...) while((s32[]{:T(128)}, ...), condition=%wide.region_8.9_spmd.clone, body=%wide.region_5.8_spmd.clone.sunk | while | flops 258776064 | bytes 10112171 | solution.py:57
  253.5 1.8 fusion.40
  260.2 1.8 fusion.40
  266.8 1.8 fusion.40
  273.5 1.8 fusion.40
  280.2 1.8 fusion.40
  286.9 1.8 fusion.40
  293.6 1.8 fusion.40
  300.2 1.8 fusion.40
  313.6 1.8 fusion.40
  320.3 1.8 fusion.40
  356.5 4.2 fusion.18
  361.9 120.9 %all-reduce.2.cloned.1.call-done = f32[1,64,1280]{2,1,0:T(8,128)} async-done(((f32[1,64,1280]{2,1,0:T(8,128)}), f32[1,64,1280]{2,1,0:T(8,128)}) %all-reduce.2.cloned.1.call-update) | async-done | bytes 327696 | tf_op jit(solution)/shard_map/psum | solution.py:109
  (91 shorter events, 64.1 us)
Async XLA Ops:
  7.2 1.3 copy-start
  7.2 125.9 %copy-start.4 = (f32[1280]{0:T(1024)S(1)}, f32[1280]{0:T(1024)}, u32[]{:S(2)}) copy-start(f32[1280]{0:T(1024)} %param.9) | copy-start | bytes 15364
  7.2 125.9 %all-gather.3.cloned.1.call-start = ((), (), s32[]{:S(2)}) async-start(), calls=%async_computation | async-start | bytes 14745600 | tf_op jit(solution)/shard_map/all_gather | solution.py:66
  7.9 347.6 %all-gather.5.cloned.1.call-start = ((), (), s32[]{:S(2)}) async-start(), calls=%async_computation.1 | async-start | bytes 4915200 | tf_op jit(solution)/shard_map/all_gather | solution.py:67
  150.3 7.9 %copy-start.3 = (s32[1,64]{1,0:T(1,128)S(1)}, s32[1,64]{1,0:T(1,128)}, u32[]{:S(2)}) copy-start(s32[1,64]{1,0:T(1,128)} %param.8) | copy-start | bytes 772
  152.2 60.8 %collective-permute-start.1 = (bf16[1,512,2,16,80]{1,4,3,2,0:T(8,128)(2,1)S(1)}, bf16[1,512,2,16,80]{1,4,3,2,0:T(8,128)(2,1)}, u32[]{:S(2)}, u32[]{:S(2)}) collective-permute-start(bf16[1,512,2,16,80]{1,4,3,2,0:T(8,128)(2,1)S(1)} %slice.17), channel_id=1, source_target_pairs={{2,0},{4,2},{6,4},{8,6},{10,8},{12,10},{14,12},{16,14},{18,16},{20... | collective-permute-start | bytes 7864328 | tf_op jit(solution)/shard_map/ppermute | solution.py:18
  154.7 87.1 %collective-permute-start = (bf16[1,512,2,16,80]{1,4,3,2,0:T(8,128)(2,1)S(1)}, bf16[1,512,2,16,80]{1,4,3,2,0:T(8,128)(2,1)}, u32[]{:S(2)}, u32[]{:S(2)}) collective-permute-start(bf16[1,512,2,16,80]{1,4,3,2,0:T(8,128)(2,1)S(1)} %slice.17), channel_id=1, source_target_pairs={{0,2},{2,4},{4,6},{6,8},{8,10},{10,12},{12,14},{14,16},{16,18},{18... | collective-permute-start | bytes 7864328 | tf_op jit(solution)/shard_map/ppermute | solution.py:15
  158.1 324.8 %all-reduce.2.cloned.1.call-start = ((), (), s32[]{:S(2)}) async-start(), calls=%async_computation.2 | async-start | bytes 655360 | tf_op jit(solution)/shard_map/psum | solution.py:109
  245.2 3.4 copy-start.5
  248.6 107.9 %copy-start.1 = (bf16[1,512,1280]{2,1,0:T(8,128)(2,1)S(1)}, bf16[1,512,1280]{2,1,0:T(8,128)(2,1)}, u32[]{:S(2)}) copy-start(bf16[1,512,1280]{2,1,0:T(8,128)(2,1)} %param.7) | copy-start | bytes 3932164
  355.5 1.1 copy-start.6
  360.8 123.9 %copy-start.2 = (bf16[1,512,1280]{2,1,0:T(8,128)(2,1)}, bf16[1,512,1280]{2,1,0:T(8,128)(2,1)S(1)}, u32[]{:S(2)}) copy-start(bf16[1,512,1280]{2,1,0:T(8,128)(2,1)S(1)} %fusion.18) | copy-start | bytes 3932164
Sparse Core Ops, SparseCore 0:
  9.6 123.4 all-gather.2
  158.2 47.8 all-gather.4
  362.1 120.7 all-reduce.1
where the time goes:
time: 493 us; the launch traced here: 491 us
  waiting for transfers between devices  326 us (66%)
  matrix products  73.3 us (15%)
  loops' own time  31.3 us (6%)
  local copies, waits for them, and re-layouts  25 us (5%)
  other arithmetic  15.6 us (3%)
  between operations  13.9 us (3%)
  starting transfers between devices  5.96 us (1%)
    all_gather x1, waiting for transfers between devices, shards(): lax.all_gather(w_qkv, 'dp', axis=0, tiled=True)  124 us
    psum x1, waiting for transfers between devices, shards(): sums = lax.psum(terms, ('sx', 'sy'))  121 us
    ppermute x1, waiting for transfers between devices, with_halo(): lax.ppermute(lax.slice_in_dim(block, 0, width, axis=dim), axis, backward)  51.9 us
    another operation x1, loops' own time, one_block(): outcome = lax.map(one_head, jnp.arange(heads, dtype=jnp.int32))  31.3 us
    dot_general x16, matrix products, one_head(): jnp.dot(probs, v_head, preferred_element_type=jnp.float32)  28.9 us
    ppermute x1, waiting for transfers between devices, with_halo(): lax.ppermute(lax.slice_in_dim(block, block.shape[dim] - width, None, axis...  28.8 us
    dot_general x16, matrix products, one_head(): jnp.dot(q_head, k_head.T, preferred_element_type=jnp.float32) * scale  28.1 us
    dot_general x1, matrix products, shards(): jnp.dot(normed.reshape(count_rows * local, width), qkv_full, preferred_el...  10.9 us
  transfers between devices with their start and end apart: 5, of which 4 were waited for; matrix products, arithmetic and copies ran while one was open for 18% of the time, Pallas kernels for 0%

commit v1 on v0

--- a/solution.py
+++ b/solution.py
@@ -106,7 +106,7 @@
     onehot = (labels[:, None] == own_list[rowidx][None, :]).astype(jnp.bfloat16)
     parts_list = [jnp.dot(onehot, hidden[rowidx], preferred_element_type=jnp.float32)]
     terms = jnp.stack(parts_list, axis=0)
-    sums = lax.psum(terms, ("sx", "sy"))
+    sums = jnp.sum(lax.all_gather(terms, ("sx", "sy")), axis=0)
     pooled = sums / lengths.astype(jnp.float32)[:, :, None]
     return (hidden, pooled)
 

time: 493 us -> 461 us (0.935)
  waiting for transfers between devices: 326 us -> 291 us
    psum x1 -> x0, waiting for transfers between devices: 121 us -> none  [shards(): sums = lax.psum(terms, ('sx', 'sy'))]
    all_gather x0 -> x1, waiting for transfers between devices: none -> 85.4 us  [shards(): sums = jnp.sum(lax.all_gather(terms, ('sx', 'sy')), axis=0)]
  transfers between devices with their start and end apart: 5 -> 5, of which waited for: 4 -> 4; matrix products, arithmetic and copies ran while one was open for 18% -> 19% of each run, Pallas kernels for 0% -> 0%
where the time goes in v1:
time: 461 us; the launch traced here: 457 us
  waiting for transfers between devices  291 us (63%)
  matrix products  73.3 us (16%)
  loops' own time  31.3 us (7%)
  local copies, waits for them, and re-layouts  25 us (5%)
  other arithmetic  17.4 us (4%)
  between operations  13.9 us (3%)
  starting transfers between devices  5.96 us (1%)
    all_gather x1, waiting for transfers between devices, shards(): lax.all_gather(w_qkv, 'dp', axis=0, tiled=True)  124 us
    all_gather x1, waiting for transfers between devices, shards(): sums = jnp.sum(lax.all_gather(terms, ('sx', 'sy')), axis=0)  85.4 us
    ppermute x1, waiting for transfers between devices, with_halo(): lax.ppermute(lax.slice_in_dim(block, 0, width, axis=dim), axis, backward)  51.9 us
    another operation x1, loops' own time, one_block(): outcome = lax.map(one_head, jnp.arange(heads, dtype=jnp.int32))  31.3 us
    dot_general x16, matrix products, one_head(): jnp.dot(probs, v_head, preferred_element_type=jnp.float32)  28.9 us
    ppermute x1, waiting for transfers between devices, with_halo(): lax.ppermute(lax.slice_in_dim(block, block.shape[dim] - width, None, axis...  28.8 us
    dot_general x16, matrix products, one_head(): jnp.dot(q_head, k_head.T, preferred_element_type=jnp.float32) * scale  28.1 us
    dot_general x1, matrix products, shards(): jnp.dot(normed.reshape(count_rows * local, width), qkv_full, preferred_el...  10.9 us
  transfers between devices with their start and end apart: 5, of which 4 were waited for; matrix products, arithmetic and copies ran while one was open for 19% of the time, Pallas kernels for 0%

profile of v1, /device:TPU:8, one launch (start us, length us, event | category | flops | bytes accessed | tf_op | source)
XLA Modules:
  0.0 457.4 jit_solution(18438258062931336821)
XLA Ops:
  9.2 123.8 %all-gather.5.cloned.1.call-done = bf16[1280,3840]{1,0:T(8,128)(2,1)} async-done(((bf16[640,3840]{1,0:T(8,128)(2,1)}), bf16[1280,3840]{1,0:T(8,128)(2,1)}) %all-gather.5.cloned.1.call-update) | async-done | bytes 9830416 | tf_op jit(solution)/shard_map/all_gather | solution.py:66
  133.0 10.9 %convolution_convert_fusion = bf16[512,3840]{1,0:T(8,128)(2,1)} fusion(bf16[1280,3840]{1,0:T(8,128)(2,1)} %all-gather.5.cloned.1.call-done, bf16[1,512,1280]{2,1,0:T(8,128)(2,1)S(1)} %copy-done, f32[1280]{0:T(1024)S(1)} %copy-done.4, f32[512]{0:T(512)S(1)} %add_rsqrt_fusion, f32[512]{0:T(512)S(1)} %broadcast_multiply_fusion), kind=kOutput, calls=%fused_computation.19 | convolution fusion | flops 5038407680 | bytes 15082496 | tf_op jit(solution)/shard_map/dot_general | solution.py:81
  144.0 6.3 %copy.10 = bf16[512,3840]{0,1:T(8,128)(2,1)} copy(bf16[512,3840]{1,0:T(8,128)(2,1)} %convolution_convert_fusion) | data formatting | bytes 7864320 | tf_op jit(solution)/shard_map/convert_element_type | solution.py:84
  150.3 1.9 slice.17
  152.2 2.5 collective-permute-start.1
  154.7 3.4 collective-permute-start
  158.7 2.5 slice_bitcast_fusion.2
  161.2 51.9 %collective-permute-done.1 = bf16[1,512,2,16,80]{1,4,3,2,0:T(8,128)(2,1)} collective-permute-done((bf16[1,512,2,16,80]{1,4,3,2,0:T(8,128)(2,1)S(1)}, bf16[1,512,2,16,80]{1,4,3,2,0:T(8,128)(2,1)}, u32[]{:S(2)}, u32[]{:S(2)}) %collective-permute-start.1) | collective-permute-done | bytes 2621472 | tf_op jit(solution)/shard_map/ppermute | solution.py:18
  213.0 28.8 %collective-permute-done = bf16[1,512,2,16,80]{1,4,3,2,0:T(8,128)(2,1)} collective-permute-done((bf16[1,512,2,16,80]{1,4,3,2,0:T(8,128)(2,1)S(1)}, bf16[1,512,2,16,80]{1,4,3,2,0:T(8,128)(2,1)}, u32[]{:S(2)}, u32[]{:S(2)}) %collective-permute-start) | collective-permute-done | bytes 2621472 | tf_op jit(solution)/shard_map/ppermute | solution.py:15
  241.8 3.4 pad_maximum_fusion
  245.3 3.4 slice_bitcast_fusion
  248.6 106.8 %while.18 = (s32[]{:T(128)}, bf16[16,512,80]{1,2,0:T(8,128)(2,1)S(1)}, s32[16]{0:T(128)S(1)}, bf16[512,16,80]{0,2,1:T(8,128)(2,1)}, bf16[1536,16,80]{0,2,1:T(8,1...) while((s32[]{:T(128)}, ...), condition=%wide.region_8.9_spmd.clone, body=%wide.region_5.8_spmd.clone.sunk | while | flops 258776064 | bytes 10112171 | solution.py:57
  253.5 1.8 fusion.41
  260.2 1.8 fusion.41
  266.8 1.8 fusion.41
  273.5 1.8 fusion.41
  280.2 1.8 fusion.41
  286.9 1.8 fusion.41
  293.6 1.8 fusion.41
  300.2 1.8 fusion.41
  313.6 1.8 fusion.41
  356.5 4.2 fusion.18
  361.9 85.4 %all-gather.9.cloned.1.call-done = f32[1024,1280]{1,0:T(8,128)} async-done(((f32[64,1280]{1,0:T(8,128)}), f32[1024,1280]{1,0:T(8,128)}) %all-gather.9.cloned.1.call-update) | async-done | bytes 5242896 | tf_op jit(solution)/shard_map/all_gather | solution.py:109
  447.3 2.8 reduce.3
  (92 shorter events, 64.9 us)
Async XLA Ops:
  7.2 1.3 copy-start
  7.2 125.9 %copy-start.4 = (f32[1280]{0:T(1024)S(1)}, f32[1280]{0:T(1024)}, u32[]{:S(2)}) copy-start(f32[1280]{0:T(1024)} %param.9) | copy-start | bytes 15364
  7.2 125.9 %all-gather.5.cloned.1.call-start = ((), (), s32[]{:S(2)}) async-start(), calls=%async_computation | async-start | bytes 14745600 | tf_op jit(solution)/shard_map/all_gather | solution.py:66
  7.9 347.6 %all-gather.7.cloned.1.call-start = ((), (), s32[]{:S(2)}) async-start(), calls=%async_computation.1 | async-start | bytes 4915200 | tf_op jit(solution)/shard_map/all_gather | solution.py:67
  150.3 7.9 %copy-start.3 = (s32[1,64]{1,0:T(1,128)S(1)}, s32[1,64]{1,0:T(1,128)}, u32[]{:S(2)}) copy-start(s32[1,64]{1,0:T(1,128)} %param.8) | copy-start | bytes 772
  152.2 60.8 %collective-permute-start.1 = (bf16[1,512,2,16,80]{1,4,3,2,0:T(8,128)(2,1)S(1)}, bf16[1,512,2,16,80]{1,4,3,2,0:T(8,128)(2,1)}, u32[]{:S(2)}, u32[]{:S(2)}) collective-permute-start(bf16[1,512,2,16,80]{1,4,3,2,0:T(8,128)(2,1)S(1)} %slice.17), channel_id=1, source_target_pairs={{2,0},{4,2},{6,4},{8,6},{10,8},{12,10},{14,12},{16,14},{18,16},{20... | collective-permute-start | bytes 7864328 | tf_op jit(solution)/shard_map/ppermute | solution.py:18
  154.7 87.1 %collective-permute-start = (bf16[1,512,2,16,80]{1,4,3,2,0:T(8,128)(2,1)S(1)}, bf16[1,512,2,16,80]{1,4,3,2,0:T(8,128)(2,1)}, u32[]{:S(2)}, u32[]{:S(2)}) collective-permute-start(bf16[1,512,2,16,80]{1,4,3,2,0:T(8,128)(2,1)S(1)} %slice.17), channel_id=1, source_target_pairs={{0,2},{2,4},{4,6},{6,8},{8,10},{10,12},{12,14},{14,16},{16,18},{18... | collective-permute-start | bytes 7864328 | tf_op jit(solution)/shard_map/ppermute | solution.py:15
  158.1 289.2 %all-gather.9.cloned.1.call-start = ((), (), s32[]{:S(2)}) async-start(), calls=%async_computation.2 | async-start | bytes 5570560 | tf_op jit(solution)/shard_map/all_gather | solution.py:109
  245.2 3.4 copy-start.5
  248.6 107.9 %copy-start.1 = (bf16[1,512,1280]{2,1,0:T(8,128)(2,1)S(1)}, bf16[1,512,1280]{2,1,0:T(8,128)(2,1)}, u32[]{:S(2)}) copy-start(bf16[1,512,1280]{2,1,0:T(8,128)(2,1)} %param.7) | copy-start | bytes 3932164
  355.5 1.1 copy-start.6
  360.8 89.3 %copy-start.2 = (bf16[1,512,1280]{2,1,0:T(8,128)(2,1)}, bf16[1,512,1280]{2,1,0:T(8,128)(2,1)S(1)}, u32[]{:S(2)}) copy-start(bf16[1,512,1280]{2,1,0:T(8,128)(2,1)S(1)} %fusion.18) | copy-start | bytes 3932164
Sparse Core Ops, SparseCore 0:
  9.6 123.4 all-gather.4
  158.2 47.8 all-gather.6
  362.1 85.2 all-gather.8
